TPU v7x, 128 devices: a whole 4x4x4 slice. The times are simulated.
128 devices in a mesh: bank: 4 (over x_hi, core), lane: 32 (over z, y, x_lo).
Axes of the slice: x: 4 (x_hi: 2, x_lo: 2; x = x_hi * 2 + x_lo), y: 4, z: 4, core: 2. Of those that a mesh axis runs over, the one named last changes fastest.
Arguments:
- amplitudes: float32 [2, 1024, 128, 128], P(None, ('bank', 'lane')), may hold values from -6 to 6
- energies: float32 [1024, 128, 128], P(('bank', 'lane')), may hold values from -2 to 2
- diagonal_angles: float32 [2, 128], replicated, may hold values from 0.3 to 1.2
Outputs:
- final_parts: float32 [2, 1024, 128, 128], P(None, ('bank', 'lane'))
- marginal: float32 [256, 128, 128], P('lane', 'bank')
All inputs are finite; a program needn't handle non-finite values.
Results may differ from a plain program's by a relative error of at most 0.0003.
Values sent between devices are 32-bit elements; how exact they have to be, the bound alone decides.
A program may use at most 64 MiB of HBM per device.

v0:
```python
import jax
import jax.numpy as jnp
from jax import lax
from jax.sharding import PartitionSpec as P

LAYERS = 2


def cut_along(shard, dim, size):
    shape = shard.shape
    parts = shard.reshape(*shape[:dim], size, shape[dim] // size, *shape[dim + 1 :])
    return jnp.moveaxis(parts, dim, 0)


def sent_and_summed(shard, axis, dim):
    size = lax.axis_size(axis)
    parts = lax.all_to_all(cut_along(shard, dim, size), axis, 0, 0, tiled=True)
    return jnp.sum(parts, axis=0)


def count_bits(values, count):
    places = jnp.arange(count.bit_length() - 1, dtype=jnp.int32)
    return jnp.sum(values[..., None] >> places & 1, axis=-1)


def walsh_table(count):
    rank = jnp.arange(count, dtype=jnp.int32)
    parity = count_bits(rank[:, None] & rank[None, :], count) % 2
    real_part = jnp.where(parity == 1, -1.0, 1.0).astype(jnp.float32) * count ** (-0.5)
    return real_part


def apply_along(values, dim):
    real_part = walsh_table(values.shape[dim])
    moved = jnp.tensordot(values, real_part, axes=([dim], [0]), precision=lax.Precision.HIGHEST)
    return jnp.moveaxis(moved, -1, dim)


def diagonal_step(values, levels, angle):
    turn = angle * levels
    return jnp.stack(
        [
            values[0] * jnp.cos(turn) + values[1] * jnp.sin(turn),
            values[1] * jnp.cos(turn) - values[0] * jnp.sin(turn),
        ]
    )


def shards(amplitudes, energies, diagonal_angles):
    values = amplitudes
    for layer in range(LAYERS):
        values = diagonal_step(values, energies, diagonal_angles[layer])
        values = apply_along(values, 3)
        values = apply_along(values, 2)
        moved = lax.all_to_all(values, "bank", split_axis=2, concat_axis=1, tiled=True)
        moved = apply_along(moved, 1)
        values = lax.all_to_all(moved, "bank", split_axis=1, concat_axis=2, tiled=True)
        moved = lax.all_to_all(values, "lane", split_axis=3, concat_axis=1, tiled=True)
        spread = moved.reshape(2, lax.axis_size("lane"), -1, moved.shape[2], moved.shape[3])
        moved = apply_along(spread, 1).reshape(moved.shape)
        values = lax.all_to_all(moved, "lane", split_axis=1, concat_axis=3, tiled=True)
    chance = values[0] * values[0] + values[1] * values[1]
    marginal = sent_and_summed(chance, "bank", 1) / lax.axis_size("bank")
    return (values, marginal)


def solution(mesh):
    return jax.shard_map(
        shards,
        mesh=mesh,
        in_specs=(P(None, ("bank", "lane"), None, None), P(("bank", "lane"), None, None), P()),
        out_specs=(P(None, ("bank", "lane"), None, None), P("lane", "bank", None)),
        check_vma=False,
    )
```

profile of v0, /device:TPU:1, one launch (start us, length us, event | category | flops | bytes accessed | tf_op | source)
XLA Modules:
  0.0 207.4 jit_solution(16305064443927837955)
XLA Ops:
  0.6 0.8 slice_bitcast_fusion
  1.5 3.1 %fusion.18 = (f32[1,8,128,128]{3,2,1,0:T(8,128)S(1)}, f32[1,8,128,128]{3,2,1,0:T(8,128)S(1)}) fusion(f32[2,8,128,128]{3,2,1,0:T(8,128)} %param.3, f32[8,128,128]{2,1,0:T(8,128)} %param.4, f32[128]{0:T(128)S(1)} %get-tuple-element.17), kind=kLoop, calls=%fused_computation.32 | loop fusion | flops 917504 | bytes 2621952 | tf_op jit(solution)/shard_map/stack | solution.py:41
  4.6 1.1 fusion
  5.7 1.0 convolution_bitcast_fusion.5
  6.7 1.4 copy.98
  8.0 5.8 %all-to-all-start = ((f32[2,8,128,128]{3,1,0,2:T(8,128)}), f32[2,8,128,128]{3,1,0,2:T(8,128)S(1)}, u32[]{:S(2)}, u32[]{:S(2)}) async-start(f32[2,8,128,128]{3,1,0,2:T(8,128)} %copy.98), calls=%async_computation | async-start | bytes 2097152 | tf_op jit(solution)/shard_map/all_to_all | solution.py:55
  13.9 14.9 %all-to-all-done = f32[2,8,128,128]{3,1,0,2:T(8,128)S(1)} async-done(((f32[2,8,128,128]{3,1,0,2:T(8,128)}), f32[2,8,128,128]{3,1,0,2:T(8,128)S(1)}, u32[]{:S(2)}, u32[]{:S(2)}) %all-to-all-start) | async-done | bytes 1048608 | tf_op jit(solution)/shard_map/all_to_all | solution.py:55
  28.8 1.0 convolution_bitcast_fusion.4
  29.8 0.6 copy.102
  30.4 18.3 %all_to_all.140 = f32[2,32,32,128]{3,2,0,1:T(8,128)S(1)} all-to-all(f32[2,32,32,128]{3,2,0,1:T(8,128)S(1)} %copy.102), channel_id=1, replica_groups=mesh['bank'=4,'lane'=32] {'bank'}, dimensions={1} | all-to-all | bytes 2097152 | tf_op jit(solution)/shard_map/all_to_all | solution.py:57
  49.3 24.5 %all_to_all.141 = f32[2,8,128,128]{2,1,0,3:T(8,128)S(1)} all-to-all(f32[2,8,128,128]{2,1,0,3:T(8,128)S(1)} %copy.105), channel_id=1, replica_groups=mesh['bank'=4,'lane'=32] {'lane'}, dimensions={3} | all-to-all | bytes 2097152 | tf_op jit(solution)/shard_map/all_to_all | solution.py:58
  73.8 1.7 convolution_bitcast_fusion.3
  76.2 0.7 copy.110
  76.8 19.5 %all_to_all.142 = f32[2,256,128,4]{2,3,0,1:T(4,128)S(1)} all-to-all(f32[2,256,128,4]{2,3,0,1:T(4,128)S(1)} %copy.110), channel_id=1, replica_groups=mesh['bank'=4,'lane'=32] {'lane'}, dimensions={1} | all-to-all | bytes 2097152 | tf_op jit(solution)/shard_map/all_to_all | solution.py:61
  97.6 2.0 add_bitcast_fusion
  99.6 1.1 fusion.4
  100.8 1.0 convolution_bitcast_fusion.2
  102.2 20.6 %all_to_all.143 = f32[2,8,128,128]{3,1,0,2:T(8,128)S(1)} all-to-all(f32[2,8,128,128]{3,1,0,2:T(8,128)S(1)} %copy.119), channel_id=1, replica_groups=mesh['bank'=4,'lane'=32] {'bank'}, dimensions={2} | all-to-all | bytes 2097152 | tf_op jit(solution)/shard_map/all_to_all | solution.py:55
  122.8 1.0 convolution_bitcast_fusion.1
  123.8 0.6 copy.123
  124.4 18.4 %all_to_all.144 = f32[2,32,32,128]{3,2,0,1:T(8,128)S(1)} all-to-all(f32[2,32,32,128]{3,2,0,1:T(8,128)S(1)} %copy.123), channel_id=1, replica_groups=mesh['bank'=4,'lane'=32] {'bank'}, dimensions={1} | all-to-all | bytes 2097152 | tf_op jit(solution)/shard_map/all_to_all | solution.py:57
  143.4 19.5 %all_to_all.145 = f32[2,8,128,128]{2,1,0,3:T(8,128)S(1)} all-to-all(f32[2,8,128,128]{2,1,0,3:T(8,128)S(1)} %copy.126), channel_id=1, replica_groups=mesh['bank'=4,'lane'=32] {'lane'}, dimensions={3} | all-to-all | bytes 2097152 | tf_op jit(solution)/shard_map/all_to_all | solution.py:58
  162.9 1.7 convolution_bitcast_fusion
  165.3 0.7 copy.131
  166.0 19.5 %all_to_all.146 = f32[2,256,128,4]{2,3,0,1:T(4,128)S(1)} all-to-all(f32[2,256,128,4]{2,3,0,1:T(4,128)S(1)} %copy.131), channel_id=1, replica_groups=mesh['bank'=4,'lane'=32] {'lane'}, dimensions={1} | all-to-all | bytes 2097152 | tf_op jit(solution)/shard_map/all_to_all | solution.py:61
  185.7 0.9 copy.134
  186.6 2.1 %add.42 = f32[8,4,32,128]{2,1,0,3:T(4,128)S(1)} reshape(f32[1,8,128,32,4]{2,1,4,3,0:T(8,128)} %copy.134) | data formatting | bytes 1048576 | tf_op jit(solution)/shard_map/add | solution.py:62
  188.6 1.6 copy.135
  190.3 6.5 %all-to-all-start.8 = ((f32[4,8,32,128]{3,2,1,0:T(8,128)}), f32[4,8,32,128]{3,2,1,0:T(8,128)S(1)}, u32[]{:S(2)}, u32[]{:S(2)}) async-start(f32[4,8,32,128]{3,2,1,0:T(8,128)} %copy.135), calls=%async_computation.8 | async-start | bytes 1048576 | tf_op jit(solution)/shard_map/all_to_all | solution.py:17
  197.0 1.4 copy.137
  198.3 7.9 %all-to-all-done.8 = f32[4,8,32,128]{3,2,1,0:T(8,128)S(1)} async-done(((f32[4,8,32,128]{3,2,1,0:T(8,128)}), f32[4,8,32,128]{3,2,1,0:T(8,128)S(1)}, u32[]{:S(2)}, u32[]{:S(2)}) %all-to-all-start.8) | async-done | bytes 524320 | tf_op jit(solution)/shard_map/all_to_all | solution.py:17
  206.5 0.9 copy.138
  (27 shorter events, 5.0 us)
Async XLA Ops:
  8.0 20.8 %all-to-all-start = ((f32[2,8,128,128]{3,1,0,2:T(8,128)}), f32[2,8,128,128]{3,1,0,2:T(8,128)S(1)}, u32[]{:S(2)}, u32[]{:S(2)}) async-start(f32[2,8,128,128]{3,1,0,2:T(8,128)} %copy.98), calls=%async_computation | async-start | bytes 2097152 | tf_op jit(solution)/shard_map/all_to_all | solution.py:55
  96.6 1.0 copy-start
  190.3 15.9 %all-to-all-start.8 = ((f32[4,8,32,128]{3,2,1,0:T(8,128)}), f32[4,8,32,128]{3,2,1,0:T(8,128)S(1)}, u32[]{:S(2)}, u32[]{:S(2)}) async-start(f32[4,8,32,128]{3,2,1,0:T(8,128)} %copy.135), calls=%async_computation.8 | async-start | bytes 1048576 | tf_op jit(solution)/shard_map/all_to_all | solution.py:17
where the time goes:
time: 208 us; the launch traced here: 207 us
  blocking collectives  140 us (67%)
  waiting for transfers between devices  22.8 us (11%)
  local copies, waits for them, and re-layouts  16.3 us (8%)
  starting transfers between devices  12.3 us (6%)
  matrix products  9.65 us (5%)
  other arithmetic  5.36 us (3%)
    all_to_all x2, blocking collectives, shards(): lax.all_to_all(values, 'lane', split_axis=3, concat_axis=1, tiled=True)  44 us
    all_to_all x2, blocking collectives, shards(): lax.all_to_all(moved, 'lane', split_axis=1, concat_axis=3, tiled=True)  38.9 us
    all_to_all x2, blocking collectives, shards(): lax.all_to_all(moved, 'bank', split_axis=1, concat_axis=2, tiled=True)  36.6 us
    all_to_all x1, blocking collectives, shards(): lax.all_to_all(values, 'bank', split_axis=2, concat_axis=1, tiled=True)  20.6 us
    all_to_all x1, waiting for transfers between devices, shards(): lax.all_to_all(values, 'bank', split_axis=2, concat_axis=1, tiled=True)  14.9 us
    dot_general x8, matrix products, apply_along(): jnp.tensordot(values, real_part, axes=([dim], [0]), precision=lax.Precisi...  9.65 us
    all_to_all x1, waiting for transfers between devices, sent_and_summed(): parts = lax.all_to_all(cut_along(shard, dim, size), axis, 0, 0, tiled=True)  7.87 us
    all_to_all x1, starting transfers between devices, sent_and_summed(): parts = lax.all_to_all(cut_along(shard, dim, size), axis, 0, 0, tiled=True)  6.53 us
  transfers between devices with their start and end apart: 2, of which 2 were waited for; matrix products, arithmetic and copies ran while one was open for 1% of the time, Pallas kernels for 0%

commit v1 on v0

v1 whole, which is shorter than its diff:
```python
import jax
import jax.numpy as jnp
from jax import lax
from jax.experimental import pallas as pl
from jax.experimental.pallas import tpu as pltpu
from jax.sharding import PartitionSpec as P

LOGICAL = pl.DeviceIdType.LOGICAL
LAYER_SCALE = 2.0**-12
SIN = (
    1.0,
    -0.1666666716337204,
    0.00833333283662796,
    -0.00019841179891955107,
    2.755283276201226e-06,
    -2.493705153483461e-08,
    1.458471399207184e-10,
)
COS = (
    1.0,
    -0.5,
    0.0416666679084301,
    -0.0013888886896893382,
    2.4801460313028656e-05,
    -2.75526161885864e-07,
    2.0779600262699205e-09,
    -1.0417342335977686e-11,
)


def polynomial(coefficients, u):
    total = jnp.full_like(u, coefficients[-1] * LAYER_SCALE)
    for c in coefficients[-2::-1]:
        total = total * u + c * LAYER_SCALE
    return total


def scaled_cos_sin(turn):
    u = turn * turn
    return polynomial(COS, u), polynomial(SIN, u) * turn


def halves(x):
    high = x.astype(jnp.bfloat16)
    low = (x - high.astype(jnp.float32)).astype(jnp.bfloat16)
    return high, low


def position():
    b, l = lax.axis_index("bank"), lax.axis_index("lane")
    x = lax.div(b, 2) * 2 + lax.rem(l, 2)
    return x, lax.rem(lax.div(l, 2), 4), lax.div(l, 8), lax.rem(b, 2)


def for_peers(visit):
    x, y, z, core = position()
    across = []
    for dx in (2, 1, 3, 0):
        xx = lax.rem(x + dx, 4)
        for dc in (1, 0):
            cc = lax.rem(core + dc, 2)
            across.append((lax.div(xx, 2) * 2 + cc) * 32 + lax.rem(xx, 2))

    def plane(t, carry):
        zz = lax.rem(z + lax.div(t, 4) + 2, 4)
        yy = lax.rem(y + lax.rem(t, 4) + 2, 4)
        for a in across:
            visit(zz * 8 + yy * 2 + a)
        return carry

    lax.fori_loop(0, 10, plane, 0)
    for a in across[:-1]:
        visit(z * 8 + y * 2 + a)
    lax.fori_loop(11, 16, plane, 0)


def kernel(
    amp_ref, en_ref, angle_ref, out_ref, marg_ref,
    a, e, eb, bt, cs, b2, a2, psi, prob, half, mine, part,
    wide, tall, load_sem, e_send, e_recv, t_send, t_recv, r_send, r_recv,
    d_send, d_recv, m_send, m_recv, out_sem,
):
    bank, lane = lax.axis_index("bank"), lax.axis_index("lane")
    me = bank * 32 + lane
    core, x_hi = lax.rem(bank, 2), lax.div(bank, 2)

    barrier = pltpu.get_barrier_semaphore()
    load_e = pltpu.make_async_copy(en_ref, e, load_sem.at[0])
    load_a = pltpu.make_async_copy(amp_ref, a, load_sem.at[1])
    load_e.start()
    load_a.start()
    for_peers(lambda d: pl.semaphore_signal(barrier, inc=1, device_id=d, device_id_type=LOGICAL))

    both = lax.broadcasted_iota(jnp.int32, (128, 256), 0) & (lax.broadcasted_iota(jnp.int32, (128, 256), 1) % 128)
    for s in (4, 2, 1):
        both = both ^ (both >> s)
    wide[...] = (1 - 2 * (both & 1)).astype(jnp.float32).astype(jnp.bfloat16)
    both = lax.broadcasted_iota(jnp.int32, (256, 128), 1) & (lax.broadcasted_iota(jnp.int32, (256, 128), 0) % 128)
    for s in (4, 2, 1):
        both = both ^ (both >> s)
    tall[...] = (1 - 2 * (both & 1)).astype(jnp.float32).astype(jnp.bfloat16)

    load_e.wait()
    pl.semaphore_wait(barrier, 127)

    for_peers(
        lambda d: pltpu.make_async_remote_copy(
            src_ref=e.at[:, :, d, :],
            dst_ref=eb.at[:, pl.ds(pl.multiple_of(me * 4, 4), 4), :],
            send_sem=e_send, recv_sem=e_recv, device_id=d, device_id_type=LOGICAL,
        ).start()
    )
    load_a.wait()

    def left(re, im):
        rh, rl = halves(re)
        ih, il = halves(im)
        rhs = jnp.concatenate(
            [jnp.concatenate([rh, ih], axis=1), jnp.concatenate([rl, il], axis=1)], axis=0
        )
        got = jnp.dot(wide[...], rhs, preferred_element_type=jnp.float32)
        return got[:, :128], got[:, 128:]

    def right(block):
        return jnp.dot(
            jnp.concatenate(halves(block), axis=1), tall[...], preferred_element_type=jnp.float32
        )

    angle = angle_ref[...]

    def first(k, carry):
        blocks = []
        for q in range(2):
            c, s = scaled_cos_sin(e[q, k] * angle[0:1, :])
            re, im = a[0, q, k], a[1, q, k]
            blocks += [re * c + im * s, im * c - re * s]
        got = right(jnp.concatenate(blocks, axis=0))
        got = [got[i * 128 : (i + 1) * 128] for i in range(4)]
        for q in range(2):
            sign = 1.0 - 2.0 * q
            re, im = left(got[0] + sign * got[2], got[1] + sign * got[3])
            a[0, q, k] = re
            a[1, q, k] = im
        return carry

    lax.fori_loop(0, 4, first, 0)

    for q in range(2):
        for_peers(
            lambda d: pltpu.make_async_remote_copy(
                src_ref=a.at[:, q, :, d, :],
                dst_ref=bt.at[q, :, pl.ds(pl.multiple_of(me * 4, 4), 4), :],
                send_sem=t_send.at[q], recv_sem=t_recv.at[q], device_id=d, device_id_type=LOGICAL,
            ).start()
        )
    for q in range(2):
        for k in range(4):
            eb[q, pl.ds(me * 4 + k, 1), :] = e[q, k, pl.ds(me, 1), :]
            for i in range(2):
                bt[q, i, pl.ds(me * 4 + k, 1), :] = a[i, q, k, pl.ds(me, 1), :]

    pltpu.make_async_copy(eb.at[:, pl.ds(0, 508)], eb.at[:, pl.ds(0, 508)], e_recv).wait()

    def turns(r, carry):
        rows = pl.ds(pl.multiple_of(r * 128, 128), 128)
        for q in range(2):
            c, s = scaled_cos_sin(eb[q, rows, :] * angle[1:2, :])
            cs[q, 0, rows, :] = c
            cs[q, 1, rows, :] = s
        return carry

    lax.fori_loop(0, 4, turns, 0)

    for q in range(2):
        pltpu.make_async_copy(bt.at[q, :, pl.ds(0, 508)], bt.at[q, :, pl.ds(0, 508)], t_recv.at[q]).wait()

        def over_rows(src, dst):
            def body(r, carry):
                rows = pl.ds(pl.multiple_of(r * 128, 128), 128)
                re, im = left(src[q, 0, rows, :], src[q, 1, rows, :])
                dst[q, 0, rows, :] = re
                dst[q, 1, rows, :] = im
                return carry

            lax.fori_loop(0, 4, body, 0)

        over_rows(bt, b2)

        def middle(r, carry):
            def four(v):
                s, d, t, u = v[0] + v[1], v[0] - v[1], v[2] + v[3], v[2] - v[3]
                return [s + t, d + u, s - t, d - u]

            rows = [pl.ds(pl.multiple_of(r * 8, 8) + 128 * h, 8) for h in range(4)]
            re = four([b2[q, 0, w, :] for w in rows])
            im = four([b2[q, 1, w, :] for w in rows])
            cc = [cs[q, 0, w, :] for w in rows]
            ss = [cs[q, 1, w, :] for w in rows]
            re, im = (
                four([x * c + y * s for x, y, c, s in zip(re, im, cc, ss)]),
                four([y * c - x * s for x, y, c, s in zip(re, im, cc, ss)]),
            )
            for h in range(4):
                bt[q, 0, rows[h], :] = re[h]
                bt[q, 1, rows[h], :] = im[h]
            return carry

        lax.fori_loop(0, 16, middle, 0, unroll=4)
        over_rows(bt, b2)

        for k in range(4):
            for_peers(
                lambda d: pltpu.make_async_remote_copy(
                    src_ref=b2.at[q, :, d * 4 + k, :],
                    dst_ref=a2.at[:, q, k, me, :],
                    send_sem=r_send.at[q, k], recv_sem=r_recv.at[q, k], device_id=d, device_id_type=LOGICAL,
                ).start()
            )
        for k in range(4):
            for i in range(2):
                a2[i, q, k, pl.ds(me, 1), :] = b2[q, i, pl.ds(me * 4 + k, 1), :]

    partner = (x_hi * 2 + 1 - core) * 32 + lane
    across = ((1 - x_hi) * 2 + core) * 32 + lane

    def to_partner(k):
        return pltpu.make_async_remote_copy(
            src_ref=prob.at[k, 1 - core], dst_ref=half.at[k],
            send_sem=d_send.at[k], recv_sem=d_recv.at[k], device_id=partner, device_id_type=LOGICAL,
        )

    def to_across(k):
        return pltpu.make_async_remote_copy(
            src_ref=mine.at[k, 1 - x_hi], dst_ref=part.at[k],
            send_sem=m_send.at[k], recv_sem=m_recv.at[k], device_id=across, device_id_type=LOGICAL,
        )

    def outs(k):
        return pltpu.make_async_copy(psi.at[:, :, k], out_ref.at[:, :, k], out_sem.at[k])

    def add_partner(k):
        to_partner(k).wait_recv()
        for h in range(2):
            mine[k, h] = prob[k, core, h] + half[k, h]
        to_across(k).start()

    for k in range(4):
        for q in range(2):
            pltpu.make_async_copy(a2.at[:, q, k, pl.ds(0, 127)], a2.at[:, q, k, pl.ds(0, 127)], r_recv.at[q, k]).wait()
        blocks = []
        for q in range(2):
            sign = 1.0 - 2.0 * q
            blocks += left(a2[0, 0, k] + sign * a2[0, 1, k], a2[1, 0, k] + sign * a2[1, 1, k])
        got = right(jnp.concatenate(blocks, axis=0))
        for q in range(2):
            re, im = got[q * 256 : q * 256 + 128], got[q * 256 + 128 : q * 256 + 256]
            psi[0, q, k] = re
            psi[1, q, k] = im
            chance = re * re + im * im
            for h in range(2):
                for c in range(2):
                    at = (h * 2 + c) * 32
                    prob[k, c, h, q] = chance[at : at + 32]
        to_partner(k).start()
        outs(k).start()
        if k:
            add_partner(k - 1)
    add_partner(3)
    for k in range(4):
        to_across(k).wait_recv()
        for q in range(2):
            marg_ref[q, k] = (mine[k, x_hi, q] + part[k, q]) * 0.25
    for k in range(4):
        to_partner(k).wait_send()
        to_across(k).wait_send()
        outs(k).wait()
    pltpu.make_async_copy(eb.at[:, pl.ds(0, 508)], eb.at[:, pl.ds(0, 508)], e_send).wait()
    for q in range(2):
        pltpu.make_async_copy(bt.at[q, :, pl.ds(0, 508)], bt.at[q, :, pl.ds(0, 508)], t_send.at[q]).wait()
        for k in range(4):
            pltpu.make_async_copy(a2.at[:, q, k, pl.ds(0, 127)], a2.at[:, q, k, pl.ds(0, 127)], r_send.at[q, k]).wait()


def shards(amplitudes, energies, angles):
    f32, bf16 = jnp.float32, jnp.bfloat16
    dma = pltpu.SemaphoreType.DMA
    out, marginal = pl.pallas_call(
        kernel,
        name="walsh",
        out_shape=(
            jax.ShapeDtypeStruct((2, 2, 4, 128, 128), f32),
            jax.ShapeDtypeStruct((2, 4, 32, 128), f32),
        ),
        in_specs=[
            pl.BlockSpec(memory_space=pl.ANY),
            pl.BlockSpec(memory_space=pl.ANY),
            pl.BlockSpec(memory_space=pltpu.VMEM),
        ],
        out_specs=(pl.BlockSpec(memory_space=pl.ANY), pl.BlockSpec(memory_space=pltpu.VMEM)),
        scratch_shapes=[
            pltpu.VMEM((2, 2, 4, 128, 128), f32),
            pltpu.VMEM((2, 4, 128, 128), f32),
            pltpu.VMEM((2, 512, 128), f32),
            pltpu.VMEM((2, 2, 512, 128), f32),
            pltpu.VMEM((2, 2, 512, 128), f32),
            pltpu.VMEM((2, 2, 512, 128), f32),
            pltpu.VMEM((2, 2, 4, 128, 128), f32),
            pltpu.VMEM((2, 2, 4, 128, 128), f32),
            pltpu.VMEM((4, 2, 2, 2, 32, 128), f32),
            pltpu.VMEM((4, 2, 2, 32, 128), f32),
            pltpu.VMEM((4, 2, 2, 32, 128), f32),
            pltpu.VMEM((4, 2, 32, 128), f32),
            pltpu.VMEM((128, 256), bf16),
            pltpu.VMEM((256, 128), bf16),
            dma((2,)), dma, dma, dma((2,)), dma((2,)), dma((2, 4)), dma((2, 4)),
            dma((4,)), dma((4,)), dma((4,)), dma((4,)), dma((4,)),
        ],
        compiler_params=pltpu.CompilerParams(
            collective_id=0, has_side_effects=True, vmem_limit_bytes=48 << 20
        ),
    )(amplitudes.reshape(2, 2, 4, 128, 128), energies.reshape(2, 4, 128, 128), angles)
    return out.reshape(2, 8, 128, 128), marginal.reshape(8, 32, 128)


def solution(mesh):
    return jax.shard_map(
        shards,
        mesh=mesh,
        in_specs=(P(None, ("bank", "lane"), None, None), P(("bank", "lane"), None, None), P()),
        out_specs=(P(None, ("bank", "lane"), None, None), P("lane", "bank", None)),
        check_vma=False,
    )
```

time: 208 us -> 58.9 us (0.28)
  blocking collectives: 140 us -> 0 us
  Pallas kernels: 0 us -> 53.5 us
  waiting for transfers between devices: 22.8 us -> 0 us
  starting transfers between devices: 12.3 us -> 0 us
  local copies, waits for them, and re-layouts: 16.3 us -> 4.56 us
  matrix products: 9.65 us -> 0 us
  other arithmetic: 5.36 us -> 0 us
    all_to_all x7 -> x0, blocking collectives: 140 us -> none  [the longest x2 44 us: shards(): lax.all_to_all(values, 'lane', split_axis=3, concat_axis=1, tiled=True)]
    pallas_call x0 -> x1, Pallas kernels: none -> 53.5 us  [shards(): pl.pallas_call(kernel, name='walsh', out_shape=(jax.ShapeDtypeStruct((2,...]
    all_to_all x2 -> x0, waiting for transfers between devices: 22.8 us -> none  [the longest x1 14.9 us: shards(): lax.all_to_all(values, 'bank', split_axis=2, concat_axis=1, tiled=True)]
    all_to_all x2 -> x0, starting transfers between devices: 12.3 us -> none  [the longest x1 6.53 us: sent_and_summed(): parts = lax.all_to_all(cut_along(shard, dim, size), axis, 0, 0, tiled=True)]
    dot_general x8 -> x0, matrix products: 9.65 us -> none  [apply_along(): jnp.tensordot(values, real_part, axes=([dim], [0]), precision=lax.Precisi...]
    transpose x7 -> x0, local copies, waits for them, and re-layouts: 5.97 us -> none  [the longest x6 4.32 us: apply_along(): return jnp.moveaxis(moved, -1, dim)]
    another operation x2 -> x0, other arithmetic: 5.09 us -> none  [diagonal_step(): jnp.stack([values[0] * jnp.cos(turn) + values[1] * jnp.sin(turn), values[...]
    add x2 -> x0, local copies, waits for them, and re-layouts: 2.94 us -> none  [shards(): chance = values[0] * values[0] + values[1] * values[1]]
  transfers between devices with their start and end apart: 2 -> 0, of which waited for: 2 -> 0; matrix products, arithmetic and copies ran while one was open for 1% -> 0% of each run, Pallas kernels for 0% -> 0%
where the time goes in v1:
time: 58.9 us; the launch traced here: 58.7 us
  Pallas kernels  53.5 us (91%)
  local copies, waits for them, and re-layouts  4.56 us (8%)
  between operations  0.65 us (1%)
    pallas_call x1, Pallas kernels, shards(): pl.pallas_call(kernel, name='walsh', out_shape=(jax.ShapeDtypeStruct((2,...  53.5 us
    unnamed x8, local copies, waits for them, and re-layouts  4.56 us

profile of v1, /device:TPU:1, one launch (start us, length us, event | category | flops | bytes accessed | tf_op | source)
XLA Modules:
  0.0 58.7 jit_solution(832624440764223798)
XLA Ops:
  0.6 0.0 copy-start.2
  0.6 0.7 %copy-done.2 = f32[2,128]{1,0:T(2,128)S(1)} copy-done((f32[2,128]{1,0:T(2,128)S(1)}, f32[2,128]{1,0:T(2,128)}, u32[]{:S(2)}) %copy-start.2) | copy-done | bytes 1048
  1.3 0.0 copy-start
  1.3 1.2 %copy-done = f32[2,8,128,128]{3,2,1,0:T(8,128)S(1)} copy-done((f32[2,8,128,128]{3,2,1,0:T(8,128)S(1)}, f32[2,8,128,128]{3,2,1,0:T(8,128)}, u32[]{:S(2)}) %copy-start) | copy-done | bytes 1048600
  2.5 0.0 copy-start.1
  2.5 1.0 %copy-done.1 = f32[8,128,128]{2,1,0:T(8,128)S(1)} copy-done((f32[8,128,128]{2,1,0:T(8,128)S(1)}, f32[8,128,128]{2,1,0:T(8,128)}, u32[]{:S(2)}) %copy-start.1) | copy-done | bytes 524312
  3.6 53.5 %walsh.1 = (f32[2,2,4,128,128]{4,3,2,1,0:T(8,128)S(1)}, f32[2,4,32,128]{3,2,1,0:T(8,128)S(1)}) custom-call(f32[2,2,4,128,128]{4,3,2,1,0:T(8,128)S(1)} %bitcast.4, f32[2,4,128,128]{3,2,1,0:T(8,128)S(1)} %bitcast.6, f32[2,128]{1,0:T(2,128)S(1)} %copy-done.2), custom_call_target="tpu_custom_call" | custom-call | tf_op jit(solution)/shard_map/walsh/pallas_call | solution.py:287
  57.0 1.0 %copy.7 = f32[2,8,128,128]{3,2,1,0:T(8,128)} copy(f32[2,8,128,128]{3,2,1,0:T(8,128)S(1)} %bitcast.5) | data formatting | bytes 2097152
  58.0 0.7 %copy.8 = f32[8,32,128]{2,1,0:T(8,128)} copy(f32[8,32,128]{2,1,0:T(8,128)S(1)} %bitcast.7) | data formatting | bytes 262144
Async XLA Ops:
  0.6 0.7 %copy-start.2 = (f32[2,128]{1,0:T(2,128)S(1)}, f32[2,128]{1,0:T(2,128)}, u32[]{:S(2)}) copy-start(f32[2,128]{1,0:T(2,128)} %angle_ref.1) | copy-start | bytes 3076
  1.3 1.2 %copy-start = (f32[2,8,128,128]{3,2,1,0:T(8,128)S(1)}, f32[2,8,128,128]{3,2,1,0:T(8,128)}, u32[]{:S(2)}) copy-start(f32[2,8,128,128]{3,2,1,0:T(8,128)} %param.3) | copy-start | bytes 3145732
  2.5 1.0 %copy-start.1 = (f32[8,128,128]{2,1,0:T(8,128)S(1)}, f32[8,128,128]{2,1,0:T(8,128)}, u32[]{:S(2)}) copy-start(f32[8,128,128]{2,1,0:T(8,128)} %param.4) | copy-start | bytes 1572868

commit v2 on v1

--- a/solution.py
+++ b/solution.py
@@ -76,9 +76,9 @@
 
 def kernel(
     amp_ref, en_ref, angle_ref, out_ref, marg_ref,
-    a, e, eb, bt, cs, b2, a2, psi, prob, half, mine, part,
+    a, e, angles, eb, bt, cs, b2, a2, prob, half, mine, part,
     wide, tall, load_sem, e_send, e_recv, t_send, t_recv, r_send, r_recv,
-    d_send, d_recv, m_send, m_recv, out_sem,
+    d_send, d_recv, m_send, m_recv,
 ):
     bank, lane = lax.axis_index("bank"), lax.axis_index("lane")
     me = bank * 32 + lane
@@ -87,7 +87,9 @@
     barrier = pltpu.get_barrier_semaphore()
     load_e = pltpu.make_async_copy(en_ref, e, load_sem.at[0])
     load_a = pltpu.make_async_copy(amp_ref, a, load_sem.at[1])
+    load_angles = pltpu.make_async_copy(angle_ref, angles, load_sem.at[2])
     load_e.start()
+    load_angles.start()
     load_a.start()
     for_peers(lambda d: pl.semaphore_signal(barrier, inc=1, device_id=d, device_id_type=LOGICAL))
 
@@ -110,6 +112,7 @@
             send_sem=e_send, recv_sem=e_recv, device_id=d, device_id_type=LOGICAL,
         ).start()
     )
+    load_angles.wait()
     load_a.wait()
 
     def left(re, im):
@@ -126,7 +129,7 @@
             jnp.concatenate(halves(block), axis=1), tall[...], preferred_element_type=jnp.float32
         )
 
-    angle = angle_ref[...]
+    angle = angles[...]
 
     def first(k, carry):
         blocks = []
@@ -235,9 +238,6 @@
             send_sem=m_send.at[k], recv_sem=m_recv.at[k], device_id=across, device_id_type=LOGICAL,
         )
 
-    def outs(k):
-        return pltpu.make_async_copy(psi.at[:, :, k], out_ref.at[:, :, k], out_sem.at[k])
-
     def add_partner(k):
         to_partner(k).wait_recv()
         for h in range(2):
@@ -254,15 +254,14 @@
         got = right(jnp.concatenate(blocks, axis=0))
         for q in range(2):
             re, im = got[q * 256 : q * 256 + 128], got[q * 256 + 128 : q * 256 + 256]
-            psi[0, q, k] = re
-            psi[1, q, k] = im
+            out_ref[0, q, k] = re
+            out_ref[1, q, k] = im
             chance = re * re + im * im
             for h in range(2):
                 for c in range(2):
                     at = (h * 2 + c) * 32
                     prob[k, c, h, q] = chance[at : at + 32]
         to_partner(k).start()
-        outs(k).start()
         if k:
             add_partner(k - 1)
     add_partner(3)
@@ -273,12 +272,20 @@
     for k in range(4):
         to_partner(k).wait_send()
         to_across(k).wait_send()
-        outs(k).wait()
     pltpu.make_async_copy(eb.at[:, pl.ds(0, 508)], eb.at[:, pl.ds(0, 508)], e_send).wait()
     for q in range(2):
         pltpu.make_async_copy(bt.at[q, :, pl.ds(0, 508)], bt.at[q, :, pl.ds(0, 508)], t_send.at[q]).wait()
         for k in range(4):
             pltpu.make_async_copy(a2.at[:, q, k, pl.ds(0, 127)], a2.at[:, q, k, pl.ds(0, 127)], r_send.at[q, k]).wait()
+
+
+def leave(values_ref, marginal_ref, out_ref, marg_ref, sem):
+    copies = [pltpu.make_async_copy(values_ref.at[i], out_ref.at[i], sem.at[i]) for i in range(2)]
+    copies.append(pltpu.make_async_copy(marginal_ref, marg_ref, sem.at[2]))
+    for copy in copies:
+        copy.start()
+    for copy in copies:
+        copy.wait()
 
 
 def shards(amplitudes, energies, angles):
@@ -292,19 +299,19 @@
             jax.ShapeDtypeStruct((2, 4, 32, 128), f32),
         ),
         in_specs=[
-            pl.BlockSpec(memory_space=pl.ANY),
-            pl.BlockSpec(memory_space=pl.ANY),
-            pl.BlockSpec(memory_space=pltpu.VMEM),
+            pl.BlockSpec(memory_space=pltpu.HBM),
+            pl.BlockSpec(memory_space=pltpu.HBM),
+            pl.BlockSpec(memory_space=pltpu.HBM),
         ],
-        out_specs=(pl.BlockSpec(memory_space=pl.ANY), pl.BlockSpec(memory_space=pltpu.VMEM)),
+        out_specs=(pl.BlockSpec(memory_space=pltpu.VMEM), pl.BlockSpec(memory_space=pltpu.VMEM)),
         scratch_shapes=[
             pltpu.VMEM((2, 2, 4, 128, 128), f32),
             pltpu.VMEM((2, 4, 128, 128), f32),
+            pltpu.VMEM((2, 128), f32),
             pltpu.VMEM((2, 512, 128), f32),
             pltpu.VMEM((2, 2, 512, 128), f32),
             pltpu.VMEM((2, 2, 512, 128), f32),
             pltpu.VMEM((2, 2, 512, 128), f32),
-            pltpu.VMEM((2, 2, 4, 128, 128), f32),
             pltpu.VMEM((2, 2, 4, 128, 128), f32),
             pltpu.VMEM((4, 2, 2, 2, 32, 128), f32),
             pltpu.VMEM((4, 2, 2, 32, 128), f32),
@@ -312,13 +319,32 @@
             pltpu.VMEM((4, 2, 32, 128), f32),
             pltpu.VMEM((128, 256), bf16),
             pltpu.VMEM((256, 128), bf16),
-            dma((2,)), dma, dma, dma((2,)), dma((2,)), dma((2, 4)), dma((2, 4)),
-            dma((4,)), dma((4,)), dma((4,)), dma((4,)), dma((4,)),
+            dma((3,)), dma, dma, dma((2,)), dma((2,)), dma((2, 4)), dma((2, 4)),
+            dma((4,)), dma((4,)), dma((4,)), dma((4,)),
         ],
         compiler_params=pltpu.CompilerParams(
             collective_id=0, has_side_effects=True, vmem_limit_bytes=48 << 20
         ),
-    )(amplitudes.reshape(2, 2, 4, 128, 128), energies.reshape(2, 4, 128, 128), angles)
+    )(
+        pltpu.with_memory_space_constraint(amplitudes.reshape(2, 2, 4, 128, 128), pltpu.HBM),
+        pltpu.with_memory_space_constraint(energies.reshape(2, 4, 128, 128), pltpu.HBM),
+        pltpu.with_memory_space_constraint(angles, pltpu.HBM),
+    )
+    out, marginal = pl.pallas_call(
+        leave,
+        name="leave",
+        out_shape=(
+            jax.ShapeDtypeStruct(out.shape, f32),
+            jax.ShapeDtypeStruct(marginal.shape, f32),
+        ),
+        in_specs=[pl.BlockSpec(memory_space=pltpu.VMEM)] * 2,
+        out_specs=[pl.BlockSpec(memory_space=pltpu.HBM)] * 2,
+        scratch_shapes=[dma((3,))],
+        compiler_params=pltpu.CompilerParams(vmem_limit_bytes=8 << 20),
+    )(
+        pltpu.with_memory_space_constraint(out, pltpu.VMEM),
+        pltpu.with_memory_space_constraint(marginal, pltpu.VMEM),
+    )
     return out.reshape(2, 8, 128, 128), marginal.reshape(8, 32, 128)
 
 

time: 58.9 us -> 55.2 us (0.937)
  local copies, waits for them, and re-layouts: 4.56 us -> 0 us
  Pallas kernels: 53.5 us -> 54.4 us
    unnamed x8 -> x0, local copies, waits for them, and re-layouts: 4.56 us -> none
    pallas_call x0 -> x1, Pallas kernels: none -> 1.03 us  [shards(): pl.pallas_call(leave, name='leave', out_shape=(jax.ShapeDtypeStruct(out.s...]
where the time goes in v2:
time: 55.2 us; the launch traced here: 55.1 us
  Pallas kernels  54.4 us (99%)
  between operations  0.64 us (1%)
    pallas_call x1, Pallas kernels, shards(): pl.pallas_call(kernel, name='walsh', out_shape=(jax.ShapeDtypeStruct((2,...  53.4 us

profile of v2, /device:TPU:1, one launch (start us, length us, event | category | flops | bytes accessed | tf_op | source)
XLA Modules:
  0.0 55.1 jit_solution(16867332227575617506)
XLA Ops:
  0.6 53.4 %walsh.1 = (f32[2,2,4,128,128]{4,3,2,1,0:T(8,128)S(1)}, f32[2,4,32,128]{3,2,1,0:T(8,128)S(1)}) custom-call(f32[2,2,4,128,128]{4,3,2,1,0:T(8,128)} %bitcast.4, f32[2,4,128,128]{3,2,1,0:T(8,128)} %bitcast.5, f32[2,128]{1,0:T(2,128)} %angle_ref.1), custom_call_target="tpu_custom_call" | custom-call | tf_op jit(solution)/shard_map/walsh/pallas_call | solution.py:294
  54.0 1.0 %leave.1 = (f32[2,2,4,128,128]{4,3,2,1,0:T(8,128)}, f32[2,4,32,128]{3,2,1,0:T(8,128)}) custom-call(f32[2,2,4,128,128]{4,3,2,1,0:T(8,128)S(1)} %get-tuple-element.6.values_ref, f32[2,4,32,128]{3,2,1,0:T(8,128)S(1)} %get-tuple-element.7.marginal_ref), custom_call_target="tpu_custom_call" | custom-call | tf_op jit(solution)/shard_map/leave/pallas_call | solution.py:333

commit v3 on v2

--- a/solution.py
+++ b/solution.py
@@ -1,3 +1,6 @@
+import collections
+import itertools
+
 import jax
 import jax.numpy as jnp
 from jax import lax
@@ -52,38 +55,70 @@
     return x, lax.rem(lax.div(l, 2), 4), lax.div(l, 8), lax.rem(b, 2)
 
 
-def for_peers(visit):
+def hops(d):
+    return min(d, 4 - d)
+
+
+def peer_offsets():
+    todo = [o for o in itertools.product(range(4), range(4), range(4), range(2)) if any(o)]
+    links = lambda ax, d: [(ax, 1)] if d == 1 else [(ax, -1)] if d == 3 else [(ax, 1), (ax, -1)]
+    load, order = collections.Counter(), []
+    while todo:
+        far = max(sum(map(hops, o[:3])) for o in todo)
+
+        def cost(o):
+            uses = [links(ax, d) for ax, d in enumerate(o[:3]) if d]
+            return sum(sum(load[u] for u in use) / len(use) for use in uses)
+
+        best = min((o for o in todo if sum(map(hops, o[:3])) == far), key=cost)
+        todo.remove(best)
+        order.append(best)
+        for ax, d in enumerate(best[:3]):
+            if d:
+                for use in links(ax, d):
+                    load[use] += hops(d) / len(links(ax, d))
+    return order
+
+
+OFFSETS = peer_offsets()
+
+
+def peers():
     x, y, z, core = position()
-    across = []
-    for dx in (2, 1, 3, 0):
-        xx = lax.rem(x + dx, 4)
-        for dc in (1, 0):
-            cc = lax.rem(core + dc, 2)
-            across.append((lax.div(xx, 2) * 2 + cc) * 32 + lax.rem(xx, 2))
-
-    def plane(t, carry):
-        zz = lax.rem(z + lax.div(t, 4) + 2, 4)
-        yy = lax.rem(y + lax.rem(t, 4) + 2, 4)
-        for a in across:
-            visit(zz * 8 + yy * 2 + a)
-        return carry
-
-    lax.fori_loop(0, 10, plane, 0)
-    for a in across[:-1]:
-        visit(z * 8 + y * 2 + a)
-    lax.fori_loop(11, 16, plane, 0)
+    xs = {}
+    for dx, dc in itertools.product(range(4), range(2)):
+        xx, cc = lax.rem(x + dx, 4), lax.rem(core + dc, 2)
+        xs[dx, dc] = (lax.div(xx, 2) * 2 + cc) * 32 + lax.rem(xx, 2)
+    ys = [lax.rem(y + d, 4) * 2 for d in range(4)]
+    zs = [lax.rem(z + d, 4) * 8 for d in range(4)]
+    return xs, ys, zs
+
+
+def for_peers(numbers, visit):
+    xs, ys, zs = numbers
+    for dx, dy, dz, dc in OFFSETS:
+        visit(xs[dx, dc] + (ys[dy] + zs[dz]))
+
+
+STEPS = 4
+
+
+def slice_of(q, step):
+    width = 4 // STEPS if q else 4
+    return list(range(step * width, (step + 1) * width))
 
 
 def kernel(
     amp_ref, en_ref, angle_ref, out_ref, marg_ref,
-    a, e, angles, eb, bt, cs, b2, a2, prob, half, mine, part,
+    a, e, angles, eb, bt, cs, b2, a2, prob, half, mine, part, last,
     wide, tall, load_sem, e_send, e_recv, t_send, t_recv, r_send, r_recv,
-    d_send, d_recv, m_send, m_recv,
+    d_send, d_recv, m_send, m_recv, l_send, l_recv,
 ):
     bank, lane = lax.axis_index("bank"), lax.axis_index("lane")
     me = bank * 32 + lane
     core, x_hi = lax.rem(bank, 2), lax.div(bank, 2)
 
+    numbers = peers()
     barrier = pltpu.get_barrier_semaphore()
     load_e = pltpu.make_async_copy(en_ref, e, load_sem.at[0])
     load_a = pltpu.make_async_copy(amp_ref, a, load_sem.at[1])
@@ -91,7 +126,7 @@
     load_e.start()
     load_angles.start()
     load_a.start()
-    for_peers(lambda d: pl.semaphore_signal(barrier, inc=1, device_id=d, device_id_type=LOGICAL))
+    for_peers(numbers, lambda d: pl.semaphore_signal(barrier, inc=1, device_id=d, device_id_type=LOGICAL))
 
     both = lax.broadcasted_iota(jnp.int32, (128, 256), 0) & (lax.broadcasted_iota(jnp.int32, (128, 256), 1) % 128)
     for s in (4, 2, 1):
@@ -105,13 +140,21 @@
     load_e.wait()
     pl.semaphore_wait(barrier, 127)
 
-    for_peers(
-        lambda d: pltpu.make_async_remote_copy(
-            src_ref=e.at[:, :, d, :],
-            dst_ref=eb.at[:, pl.ds(pl.multiple_of(me * 4, 4), 4), :],
-            send_sem=e_send, recv_sem=e_recv, device_id=d, device_id_type=LOGICAL,
-        ).start()
-    )
+    def send_energies(q):
+        for_peers(
+            numbers,
+            lambda d: pltpu.make_async_remote_copy(
+                src_ref=e.at[q, :, d, :],
+                dst_ref=eb.at[q, pl.ds(pl.multiple_of(me * 4, 4), 4), :],
+                send_sem=e_send.at[q], recv_sem=e_recv.at[q], device_id=d, device_id_type=LOGICAL,
+            ).start()
+        )
+
+    def energies_done(q, sem):
+        rows = eb.at[q, pl.ds(0, 508)]
+        return pltpu.make_async_copy(rows, rows, sem.at[q])
+
+    send_energies(0)
     load_angles.wait()
     load_a.wait()
 
@@ -149,7 +192,10 @@
     lax.fori_loop(0, 4, first, 0)
 
     for q in range(2):
+        if q:
+            send_energies(1)
         for_peers(
+            numbers,
             lambda d: pltpu.make_async_remote_copy(
                 src_ref=a.at[:, q, :, d, :],
                 dst_ref=bt.at[q, :, pl.ds(pl.multiple_of(me * 4, 4), 4), :],
@@ -162,30 +208,25 @@
             for i in range(2):
                 bt[q, i, pl.ds(me * 4 + k, 1), :] = a[i, q, k, pl.ds(me, 1), :]
 
-    pltpu.make_async_copy(eb.at[:, pl.ds(0, 508)], eb.at[:, pl.ds(0, 508)], e_recv).wait()
-
-    def turns(r, carry):
-        rows = pl.ds(pl.multiple_of(r * 128, 128), 128)
-        for q in range(2):
+    for q in range(2):
+        energies_done(q, e_recv).wait()
+
+        def turns(r, carry):
+            rows = pl.ds(pl.multiple_of(r * 64, 64), 64)
             c, s = scaled_cos_sin(eb[q, rows, :] * angle[1:2, :])
             cs[q, 0, rows, :] = c
             cs[q, 1, rows, :] = s
-        return carry
-
-    lax.fori_loop(0, 4, turns, 0)
-
-    for q in range(2):
+            return carry
+
+        lax.fori_loop(0, 8, turns, 0)
         pltpu.make_async_copy(bt.at[q, :, pl.ds(0, 508)], bt.at[q, :, pl.ds(0, 508)], t_recv.at[q]).wait()
 
         def over_rows(src, dst):
-            def body(r, carry):
-                rows = pl.ds(pl.multiple_of(r * 128, 128), 128)
+            for r in range(4):
+                rows = slice(r * 128, (r + 1) * 128)
                 re, im = left(src[q, 0, rows, :], src[q, 1, rows, :])
                 dst[q, 0, rows, :] = re
                 dst[q, 1, rows, :] = im
-                return carry
-
-            lax.fori_loop(0, 4, body, 0)
 
         over_rows(bt, b2)
 
@@ -211,18 +252,25 @@
         lax.fori_loop(0, 16, middle, 0, unroll=4)
         over_rows(bt, b2)
 
-        for k in range(4):
+        for step in range(STEPS if q else 1):
+            ks = slice_of(q, step)
             for_peers(
+                numbers,
                 lambda d: pltpu.make_async_remote_copy(
-                    src_ref=b2.at[q, :, d * 4 + k, :],
-                    dst_ref=a2.at[:, q, k, me, :],
-                    send_sem=r_send.at[q, k], recv_sem=r_recv.at[q, k], device_id=d, device_id_type=LOGICAL,
+                    src_ref=b2.at[q, :, pl.ds(d * 4 + ks[0], len(ks)), :],
+                    dst_ref=a2.at[:, q, ks[0] : ks[0] + len(ks), me, :],
+                    send_sem=r_send.at[q, step], recv_sem=r_recv.at[q, step], device_id=d, device_id_type=LOGICAL,
                 ).start()
             )
         for k in range(4):
             for i in range(2):
                 a2[i, q, k, pl.ds(me, 1), :] = b2[q, i, pl.ds(me * 4 + k, 1), :]
 
+    def returned(q, step, sem):
+        ks = slice_of(q, step)
+        rows = a2.at[:, q, ks[0] : ks[0] + len(ks), pl.ds(0, 127)]
+        return pltpu.make_async_copy(rows, rows, sem.at[q, step])
+
     partner = (x_hi * 2 + 1 - core) * 32 + lane
     across = ((1 - x_hi) * 2 + core) * 32 + lane
 
@@ -236,6 +284,15 @@
         return pltpu.make_async_remote_copy(
             src_ref=mine.at[k, 1 - x_hi], dst_ref=part.at[k],
             send_sem=m_send.at[k], recv_sem=m_recv.at[k], device_id=across, device_id_type=LOGICAL,
+        )
+
+    def direct(other):
+        c = lax.rem(core + other, 2)
+        h = lax.rem(x_hi + other // 2, 2)
+        return pltpu.make_async_remote_copy(
+            src_ref=prob.at[3, c, h], dst_ref=last.at[other - 1],
+            send_sem=l_send.at[other - 1], recv_sem=l_recv.at[other - 1],
+            device_id=(h * 2 + c) * 32 + lane, device_id_type=LOGICAL,
         )
 
     def add_partner(k):
@@ -245,8 +302,10 @@
         to_across(k).start()
 
     for k in range(4):
-        for q in range(2):
-            pltpu.make_async_copy(a2.at[:, q, k, pl.ds(0, 127)], a2.at[:, q, k, pl.ds(0, 127)], r_recv.at[q, k]).wait()
+        if k == 0:
+            returned(0, 0, r_recv).wait()
+        if k % (4 // STEPS) == 0:
+            returned(1, k // (4 // STEPS), r_recv).wait()
         blocks = []
         for q in range(2):
             sign = 1.0 - 2.0 * q
@@ -261,22 +320,30 @@
                 for c in range(2):
                     at = (h * 2 + c) * 32
                     prob[k, c, h, q] = chance[at : at + 32]
-        to_partner(k).start()
+        if k < 3:
+            to_partner(k).start()
+        else:
+            for other in (2, 3, 1):
+                direct(other).start()
         if k:
             add_partner(k - 1)
-    add_partner(3)
-    for k in range(4):
+    for k in range(3):
         to_across(k).wait_recv()
         for q in range(2):
             marg_ref[q, k] = (mine[k, x_hi, q] + part[k, q]) * 0.25
-    for k in range(4):
+    for other in (1, 2, 3):
+        direct(other).wait_recv()
+    for q in range(2):
+        marg_ref[q, 3] = ((prob[3, core, x_hi, q] + last[0, q]) + (last[1, q] + last[2, q])) * 0.25
+    for k in range(3):
         to_partner(k).wait_send()
         to_across(k).wait_send()
-    pltpu.make_async_copy(eb.at[:, pl.ds(0, 508)], eb.at[:, pl.ds(0, 508)], e_send).wait()
+        direct(k + 1).wait_send()
     for q in range(2):
+        energies_done(q, e_send).wait()
         pltpu.make_async_copy(bt.at[q, :, pl.ds(0, 508)], bt.at[q, :, pl.ds(0, 508)], t_send.at[q]).wait()
-        for k in range(4):
-            pltpu.make_async_copy(a2.at[:, q, k, pl.ds(0, 127)], a2.at[:, q, k, pl.ds(0, 127)], r_send.at[q, k]).wait()
+        for step in range(STEPS if q else 1):
+            returned(q, step, r_send).wait()
 
 
 def leave(values_ref, marginal_ref, out_ref, marg_ref, sem):
@@ -314,13 +381,14 @@
             pltpu.VMEM((2, 2, 512, 128), f32),
             pltpu.VMEM((2, 2, 4, 128, 128), f32),
             pltpu.VMEM((4, 2, 2, 2, 32, 128), f32),
-            pltpu.VMEM((4, 2, 2, 32, 128), f32),
-            pltpu.VMEM((4, 2, 2, 32, 128), f32),
-            pltpu.VMEM((4, 2, 32, 128), f32),
+            pltpu.VMEM((3, 2, 2, 32, 128), f32),
+            pltpu.VMEM((3, 2, 2, 32, 128), f32),
+            pltpu.VMEM((3, 2, 32, 128), f32),
+            pltpu.VMEM((3, 2, 32, 128), f32),
             pltpu.VMEM((128, 256), bf16),
             pltpu.VMEM((256, 128), bf16),
-            dma((3,)), dma, dma, dma((2,)), dma((2,)), dma((2, 4)), dma((2, 4)),
-            dma((4,)), dma((4,)), dma((4,)), dma((4,)),
+            dma((3,)), dma((2,)), dma((2,)), dma((2,)), dma((2,)), dma((2, 4)), dma((2, 4)),
+            dma((3,)), dma((3,)), dma((3,)), dma((3,)), dma((3,)), dma((3,)),
         ],
         compiler_params=pltpu.CompilerParams(
             collective_id=0, has_side_effects=True, vmem_limit_bytes=48 << 20

time: 55.2 us -> 51.6 us (0.935)
  Pallas kernels: 54.4 us -> 50.9 us
    pallas_call x1, Pallas kernels: 53.4 us -> 49.9 us  [shards(): pl.pallas_call(kernel, name='walsh', out_shape=(jax.ShapeDtypeStruct((2,...]
where the time goes in v3:
time: 51.6 us; the launch traced here: 51.5 us
  Pallas kernels  50.9 us (99%)
  between operations  0.64 us (1%)
    pallas_call x1, Pallas kernels, shards(): pl.pallas_call(kernel, name='walsh', out_shape=(jax.ShapeDtypeStruct((2,...  49.9 us

profile of v3, /device:TPU:1, one launch (start us, length us, event | category | flops | bytes accessed | tf_op | source)
XLA Modules:
  0.0 51.5 jit_solution(1860357999171692131)
XLA Ops:
  0.6 49.9 %walsh.1 = (f32[2,2,4,128,128]{4,3,2,1,0:T(8,128)S(1)}, f32[2,4,32,128]{3,2,1,0:T(8,128)S(1)}) custom-call(f32[2,2,4,128,128]{4,3,2,1,0:T(8,128)} %bitcast.4, f32[2,4,128,128]{3,2,1,0:T(8,128)} %bitcast.5, f32[2,128]{1,0:T(2,128)} %angle_ref.1), custom_call_target="tpu_custom_call" | custom-call | tf_op jit(solution)/shard_map/walsh/pallas_call | solution.py:361
  50.5 1.0 %leave.1 = (f32[2,2,4,128,128]{4,3,2,1,0:T(8,128)}, f32[2,4,32,128]{3,2,1,0:T(8,128)}) custom-call(f32[2,2,4,128,128]{4,3,2,1,0:T(8,128)S(1)} %get-tuple-element.6.values_ref, f32[2,4,32,128]{3,2,1,0:T(8,128)S(1)} %get-tuple-element.7.marginal_ref), custom_call_target="tpu_custom_call" | custom-call | tf_op jit(solution)/shard_map/leave/pallas_call | solution.py:401

commit v4 on v3

--- a/solution.py
+++ b/solution.py
@@ -137,8 +137,6 @@
         both = both ^ (both >> s)
     tall[...] = (1 - 2 * (both & 1)).astype(jnp.float32).astype(jnp.bfloat16)
 
-    load_e.wait()
-    pl.semaphore_wait(barrier, 127)
 
     def send_energies(q):
         for_peers(
@@ -154,7 +152,7 @@
         rows = eb.at[q, pl.ds(0, 508)]
         return pltpu.make_async_copy(rows, rows, sem.at[q])
 
-    send_energies(0)
+    load_e.wait()
     load_angles.wait()
     load_a.wait()
 
@@ -190,10 +188,10 @@
         return carry
 
     lax.fori_loop(0, 4, first, 0)
+    pl.semaphore_wait(barrier, 127)
 
     for q in range(2):
-        if q:
-            send_energies(1)
+        send_energies(q)
         for_peers(
             numbers,
             lambda d: pltpu.make_async_remote_copy(

time: 51.6 us -> 49.2 us (0.953)
  Pallas kernels: 50.9 us -> 48.5 us
    pallas_call x1, Pallas kernels: 49.9 us -> 47.4 us  [shards(): pl.pallas_call(kernel, name='walsh', out_shape=(jax.ShapeDtypeStruct((2,...]
where the time goes in v4:
time: 49.2 us; the launch traced here: 49.1 us
  Pallas kernels  48.5 us (99%)
  between operations  0.64 us (1%)
    pallas_call x1, Pallas kernels, shards(): pl.pallas_call(kernel, name='walsh', out_shape=(jax.ShapeDtypeStruct((2,...  47.4 us
    pallas_call x1, Pallas kernels, shards(): pl.pallas_call(leave, name='leave', out_shape=(jax.ShapeDtypeStruct(out.s...  1.03 us

profile of v4, /device:TPU:1, one launch (start us, length us, event | category | flops | bytes accessed | tf_op | source)
XLA Modules:
  0.0 49.1 jit_solution(14954856993606760321)
XLA Ops:
  0.6 47.4 %walsh.1 = (f32[2,2,4,128,128]{4,3,2,1,0:T(8,128)S(1)}, f32[2,4,32,128]{3,2,1,0:T(8,128)S(1)}) custom-call(f32[2,2,4,128,128]{4,3,2,1,0:T(8,128)} %bitcast.4, f32[2,4,128,128]{3,2,1,0:T(8,128)} %bitcast.5, f32[2,128]{1,0:T(2,128)} %angle_ref.1), custom_call_target="tpu_custom_call" | custom-call | tf_op jit(solution)/shard_map/walsh/pallas_call | solution.py:359
  48.1 1.0 %leave.1 = (f32[2,2,4,128,128]{4,3,2,1,0:T(8,128)}, f32[2,4,32,128]{3,2,1,0:T(8,128)}) custom-call(f32[2,2,4,128,128]{4,3,2,1,0:T(8,128)S(1)} %get-tuple-element.6.values_ref, f32[2,4,32,128]{3,2,1,0:T(8,128)S(1)} %get-tuple-element.7.marginal_ref), custom_call_target="tpu_custom_call" | custom-call | tf_op jit(solution)/shard_map/leave/pallas_call | solution.py:399

commit v5 on v4

--- a/solution.py
+++ b/solution.py
@@ -100,19 +100,30 @@
         visit(xs[dx, dc] + (ys[dy] + zs[dz]))
 
 
-STEPS = 4
-
-
-def slice_of(q, step):
-    width = 4 // STEPS if q else 4
-    return list(range(step * width, (step + 1) * width))
+ORDER = [(1, 1), (1, 0), (0, 1), (0, 0)]
+
+
+def leading(bank, step):
+    dh, dc = ORDER[step]
+    return lax.rem(lax.div(bank, 2) + dh, 2) * 2 + lax.rem(lax.rem(bank, 2) + dc, 2)
+
+
+STARTS = [0, 1, 2]
+
+
+def width_of(step):
+    return 1 if step + 1 in STARTS or step == 3 else 2
+
+
+def first_of_pair(bank, step):
+    return lax.rem(lax.div(bank, 2) + ORDER[step][0], 2) * 2
 
 
 def kernel(
     amp_ref, en_ref, angle_ref, out_ref, marg_ref,
-    a, e, angles, eb, bt, cs, b2, a2, prob, half, mine, part, last,
+    a_parts, e_parts, angles, eb, bt, cs, b2, a2, prob, half, mine, part,
     wide, tall, load_sem, e_send, e_recv, t_send, t_recv, r_send, r_recv,
-    d_send, d_recv, m_send, m_recv, l_send, l_recv,
+    d_send, d_recv, m_send, m_recv,
 ):
     bank, lane = lax.axis_index("bank"), lax.axis_index("lane")
     me = bank * 32 + lane
@@ -120,12 +131,16 @@
 
     numbers = peers()
     barrier = pltpu.get_barrier_semaphore()
-    load_e = pltpu.make_async_copy(en_ref, e, load_sem.at[0])
-    load_a = pltpu.make_async_copy(amp_ref, a, load_sem.at[1])
-    load_angles = pltpu.make_async_copy(angle_ref, angles, load_sem.at[2])
-    load_e.start()
+    a, e = a_parts.reshape(2, 2, 4, 128, 128), e_parts.reshape(2, 4, 128, 128)
+    loads = []
+    for t in range(4):
+        rows = pl.ds(t * 32, 32)
+        loads.append(pltpu.make_async_copy(en_ref.at[:, :, rows, :], e_parts.at[:, t], load_sem.at[0, t]))
+        loads.append(pltpu.make_async_copy(amp_ref.at[:, :, :, rows, :], a_parts.at[:, :, t], load_sem.at[1, t]))
+    load_angles = pltpu.make_async_copy(angle_ref, angles, load_sem.at[2, 0])
     load_angles.start()
-    load_a.start()
+    for load in loads:
+        load.start()
     for_peers(numbers, lambda d: pl.semaphore_signal(barrier, inc=1, device_id=d, device_id_type=LOGICAL))
 
     both = lax.broadcasted_iota(jnp.int32, (128, 256), 0) & (lax.broadcasted_iota(jnp.int32, (128, 256), 1) % 128)
@@ -152,9 +167,9 @@
         rows = eb.at[q, pl.ds(0, 508)]
         return pltpu.make_async_copy(rows, rows, sem.at[q])
 
-    load_e.wait()
     load_angles.wait()
-    load_a.wait()
+    for load in loads:
+        load.wait()
 
     def left(re, im):
         rh, rl = halves(re)
@@ -206,6 +221,15 @@
             for i in range(2):
                 bt[q, i, pl.ds(me * 4 + k, 1), :] = a[i, q, k, pl.ds(me, 1), :]
 
+    def returned(q, step, sem):
+        if q == 0:
+            rows = a2.at[:, 0, :, pl.ds(0, 127)]
+        elif width_of(step) == 1:
+            rows = a2.at[:, 1, leading(bank, step), pl.ds(0, 127)]
+        else:
+            rows = a2.at[:, 1, pl.ds(first_of_pair(bank, step), 2), pl.ds(0, 127)]
+        return pltpu.make_async_copy(rows, rows, sem.at[q, step])
+
     for q in range(2):
         energies_done(q, e_recv).wait()
 
@@ -250,98 +274,84 @@
         lax.fori_loop(0, 16, middle, 0, unroll=4)
         over_rows(bt, b2)
 
-        for step in range(STEPS if q else 1):
-            ks = slice_of(q, step)
+        if q == 0:
             for_peers(
                 numbers,
                 lambda d: pltpu.make_async_remote_copy(
-                    src_ref=b2.at[q, :, pl.ds(d * 4 + ks[0], len(ks)), :],
-                    dst_ref=a2.at[:, q, ks[0] : ks[0] + len(ks), me, :],
-                    send_sem=r_send.at[q, step], recv_sem=r_recv.at[q, step], device_id=d, device_id_type=LOGICAL,
+                    src_ref=b2.at[0, :, pl.ds(d * 4, 4), :], dst_ref=a2.at[:, 0, :, me, :],
+                    send_sem=r_send.at[0, 0], recv_sem=r_recv.at[0, 0], device_id=d, device_id_type=LOGICAL,
                 ).start()
             )
+        else:
+            for step in STARTS:
+                wide_step = width_of(step)
+                banks = {
+                    k: leading(lax.div(v, 32), step) if wide_step == 1 else first_of_pair(lax.div(v, 32), step)
+                    for k, v in numbers[0].items()
+                }
+                xs, ys, zs = numbers
+                for dx, dy, dz, dc in OFFSETS:
+                    d, t = xs[dx, dc] + (ys[dy] + zs[dz]), banks[dx, dc]
+                    pltpu.make_async_remote_copy(
+                        src_ref=b2.at[1, :, pl.ds(d * 4 + t, wide_step), :], dst_ref=a2.at[:, 1, pl.ds(t, wide_step), me, :],
+                        send_sem=r_send.at[1, step], recv_sem=r_recv.at[1, step], device_id=d, device_id_type=LOGICAL,
+                    ).start()
         for k in range(4):
             for i in range(2):
                 a2[i, q, k, pl.ds(me, 1), :] = b2[q, i, pl.ds(me * 4 + k, 1), :]
 
-    def returned(q, step, sem):
-        ks = slice_of(q, step)
-        rows = a2.at[:, q, ks[0] : ks[0] + len(ks), pl.ds(0, 127)]
-        return pltpu.make_async_copy(rows, rows, sem.at[q, step])
-
     partner = (x_hi * 2 + 1 - core) * 32 + lane
     across = ((1 - x_hi) * 2 + core) * 32 + lane
 
-    def to_partner(k):
+    def to_partner(n):
         return pltpu.make_async_remote_copy(
-            src_ref=prob.at[k, 1 - core], dst_ref=half.at[k],
-            send_sem=d_send.at[k], recv_sem=d_recv.at[k], device_id=partner, device_id_type=LOGICAL,
-        )
-
-    def to_across(k):
+            src_ref=prob.at[2 * n], dst_ref=half.at[n],
+            send_sem=d_send.at[n], recv_sem=d_recv.at[n], device_id=partner, device_id_type=LOGICAL,
+        )
+
+    def to_across(q):
         return pltpu.make_async_remote_copy(
-            src_ref=mine.at[k, 1 - x_hi], dst_ref=part.at[k],
-            send_sem=m_send.at[k], recv_sem=m_recv.at[k], device_id=across, device_id_type=LOGICAL,
-        )
-
-    def direct(other):
-        c = lax.rem(core + other, 2)
-        h = lax.rem(x_hi + other // 2, 2)
-        return pltpu.make_async_remote_copy(
-            src_ref=prob.at[3, c, h], dst_ref=last.at[other - 1],
-            send_sem=l_send.at[other - 1], recv_sem=l_recv.at[other - 1],
-            device_id=(h * 2 + c) * 32 + lane, device_id_type=LOGICAL,
-        )
-
-    def add_partner(k):
-        to_partner(k).wait_recv()
-        for h in range(2):
-            mine[k, h] = prob[k, core, h] + half[k, h]
-        to_across(k).start()
-
-    for k in range(4):
-        if k == 0:
-            returned(0, 0, r_recv).wait()
-        if k % (4 // STEPS) == 0:
-            returned(1, k // (4 // STEPS), r_recv).wait()
-        blocks = []
+            src_ref=mine.at[q], dst_ref=part.at[q],
+            send_sem=m_send.at[q], recv_sem=m_recv.at[q], device_id=across, device_id_type=LOGICAL,
+        )
+
+    returned(0, 0, r_recv).wait()
+    for step in range(4):
+        t = leading(bank, step)
+        rows = pl.ds(pl.multiple_of(t * 32, 32), 32)
+        if step in STARTS:
+            returned(1, step, r_recv).wait()
         for q in range(2):
             sign = 1.0 - 2.0 * q
-            blocks += left(a2[0, 0, k] + sign * a2[0, 1, k], a2[1, 0, k] + sign * a2[1, 1, k])
-        got = right(jnp.concatenate(blocks, axis=0))
-        for q in range(2):
-            re, im = got[q * 256 : q * 256 + 128], got[q * 256 + 128 : q * 256 + 256]
-            out_ref[0, q, k] = re
-            out_ref[1, q, k] = im
+            re, im = left(a2[0, 0, t] + sign * a2[0, 1, t], a2[1, 0, t] + sign * a2[1, 1, t])
+            got = right(jnp.concatenate([re, im], axis=0))
+            re, im = got[:128], got[128:]
             chance = re * re + im * im
-            for h in range(2):
-                for c in range(2):
-                    at = (h * 2 + c) * 32
-                    prob[k, c, h, q] = chance[at : at + 32]
-        if k < 3:
-            to_partner(k).start()
-        else:
-            for other in (2, 3, 1):
-                direct(other).start()
-        if k:
-            add_partner(k - 1)
-    for k in range(3):
-        to_across(k).wait_recv()
-        for q in range(2):
-            marg_ref[q, k] = (mine[k, x_hi, q] + part[k, q]) * 0.25
-    for other in (1, 2, 3):
-        direct(other).wait_recv()
-    for q in range(2):
-        marg_ref[q, 3] = ((prob[3, core, x_hi, q] + last[0, q]) + (last[1, q] + last[2, q])) * 0.25
-    for k in range(3):
-        to_partner(k).wait_send()
-        to_across(k).wait_send()
-        direct(k + 1).wait_send()
+            for k in range(4):
+                at = slice(k * 32, (k + 1) * 32)
+                out_ref[0, q, k, rows, :] = re[at]
+                out_ref[1, q, k, rows, :] = im[at]
+                prob[step, q, k] = chance[at]
+            if step == 1:
+                if q == 0:
+                    to_partner(0).wait_recv()
+                mine[q] = prob[1, q] + half[0, q]
+                to_across(q).start()
+        if step in (0, 2):
+            to_partner(step // 2).start()
+    to_partner(1).wait_recv()
+    for q in range(2):
+        to_across(q).wait_recv()
+        marg_ref[q] = ((prob[3, q] + half[1, q]) + part[q]) * 0.25
+    for q in range(2):
+        to_partner(q).wait_send()
+        to_across(q).wait_send()
+    returned(0, 0, r_send).wait()
+    for step in STARTS:
+        returned(1, step, r_send).wait()
     for q in range(2):
         energies_done(q, e_send).wait()
         pltpu.make_async_copy(bt.at[q, :, pl.ds(0, 508)], bt.at[q, :, pl.ds(0, 508)], t_send.at[q]).wait()
-        for step in range(STEPS if q else 1):
-            returned(q, step, r_send).wait()
 
 
 def leave(values_ref, marginal_ref, out_ref, marg_ref, sem):
@@ -370,23 +380,22 @@
         ],
         out_specs=(pl.BlockSpec(memory_space=pltpu.VMEM), pl.BlockSpec(memory_space=pltpu.VMEM)),
         scratch_shapes=[
-            pltpu.VMEM((2, 2, 4, 128, 128), f32),
-            pltpu.VMEM((2, 4, 128, 128), f32),
+            pltpu.VMEM((2, 2, 4, 4, 32, 128), f32),
+            pltpu.VMEM((2, 4, 4, 32, 128), f32),
             pltpu.VMEM((2, 128), f32),
             pltpu.VMEM((2, 512, 128), f32),
             pltpu.VMEM((2, 2, 512, 128), f32),
             pltpu.VMEM((2, 2, 512, 128), f32),
             pltpu.VMEM((2, 2, 512, 128), f32),
             pltpu.VMEM((2, 2, 4, 128, 128), f32),
-            pltpu.VMEM((4, 2, 2, 2, 32, 128), f32),
-            pltpu.VMEM((3, 2, 2, 32, 128), f32),
-            pltpu.VMEM((3, 2, 2, 32, 128), f32),
-            pltpu.VMEM((3, 2, 32, 128), f32),
-            pltpu.VMEM((3, 2, 32, 128), f32),
+            pltpu.VMEM((4, 2, 4, 32, 128), f32),
+            pltpu.VMEM((2, 2, 4, 32, 128), f32),
+            pltpu.VMEM((2, 4, 32, 128), f32),
+            pltpu.VMEM((2, 4, 32, 128), f32),
             pltpu.VMEM((128, 256), bf16),
             pltpu.VMEM((256, 128), bf16),
-            dma((3,)), dma((2,)), dma((2,)), dma((2,)), dma((2,)), dma((2, 4)), dma((2, 4)),
-            dma((3,)), dma((3,)), dma((3,)), dma((3,)), dma((3,)), dma((3,)),
+            dma((3, 4)), dma((2,)), dma((2,)), dma((2,)), dma((2,)), dma((2, 4)), dma((2, 4)),
+            dma((2,)), dma((2,)), dma((2,)), dma((2,)),
         ],
         compiler_params=pltpu.CompilerParams(
             collective_id=0, has_side_effects=True, vmem_limit_bytes=48 << 20

time: 49.2 us -> 48.9 us (level)
  no operation moved by 1% of the time
where the time goes in v5:
time: 48.9 us; the launch traced here: 48.7 us
  Pallas kernels  48.1 us (98%)
  between operations  0.64 us (1%)
    pallas_call x1, Pallas kernels, shards(): pl.pallas_call(kernel, name='walsh', out_shape=(jax.ShapeDtypeStruct((2,...  47.1 us
    pallas_call x1, Pallas kernels, shards(): pl.pallas_call(leave, name='leave', out_shape=(jax.ShapeDtypeStruct(out.s...  1.03 us

profile of v5, /device:TPU:1, one launch (start us, length us, event | category | flops | bytes accessed | tf_op | source)
XLA Modules:
  0.0 48.7 jit_solution(3649572260396216494)
XLA Ops:
  0.6 47.1 %walsh.1 = (f32[2,2,4,128,128]{4,3,2,1,0:T(8,128)S(1)}, f32[2,4,32,128]{3,2,1,0:T(8,128)S(1)}) custom-call(f32[2,2,4,128,128]{4,3,2,1,0:T(8,128)} %bitcast.4, f32[2,4,128,128]{3,2,1,0:T(8,128)} %bitcast.5, f32[2,128]{1,0:T(2,128)} %angle_ref.1), custom_call_target="tpu_custom_call" | custom-call | tf_op jit(solution)/shard_map/walsh/pallas_call | solution.py:369
  47.7 1.0 %leave.1 = (f32[2,2,4,128,128]{4,3,2,1,0:T(8,128)}, f32[2,4,32,128]{3,2,1,0:T(8,128)}) custom-call(f32[2,2,4,128,128]{4,3,2,1,0:T(8,128)S(1)} %get-tuple-element.6.values_ref, f32[2,4,32,128]{3,2,1,0:T(8,128)S(1)} %get-tuple-element.7.marginal_ref), custom_call_target="tpu_custom_call" | custom-call | tf_op jit(solution)/shard_map/leave/pallas_call | solution.py:408

commit v6 on v5

--- a/solution.py
+++ b/solution.py
@@ -168,8 +168,6 @@
         return pltpu.make_async_copy(rows, rows, sem.at[q])
 
     load_angles.wait()
-    for load in loads:
-        load.wait()
 
     def left(re, im):
         rh, rl = halves(re)
@@ -202,7 +200,10 @@
             a[1, q, k] = im
         return carry
 
-    lax.fori_loop(0, 4, first, 0)
+    for k in range(4):
+        loads[2 * k].wait()
+        loads[2 * k + 1].wait()
+        first(k, 0)
     pl.semaphore_wait(barrier, 127)
 
     for q in range(2):
@@ -303,10 +304,10 @@
     partner = (x_hi * 2 + 1 - core) * 32 + lane
     across = ((1 - x_hi) * 2 + core) * 32 + lane
 
-    def to_partner(n):
+    def to_partner(n, q):
         return pltpu.make_async_remote_copy(
-            src_ref=prob.at[2 * n], dst_ref=half.at[n],
-            send_sem=d_send.at[n], recv_sem=d_recv.at[n], device_id=partner, device_id_type=LOGICAL,
+            src_ref=prob.at[2 * n, q], dst_ref=half.at[n, q],
+            send_sem=d_send.at[n, q], recv_sem=d_recv.at[n, q], device_id=partner, device_id_type=LOGICAL,
         )
 
     def to_across(q):
@@ -332,19 +333,19 @@
                 out_ref[0, q, k, rows, :] = re[at]
                 out_ref[1, q, k, rows, :] = im[at]
                 prob[step, q, k] = chance[at]
+            if step in (0, 2):
+                to_partner(step // 2, q).start()
             if step == 1:
-                if q == 0:
-                    to_partner(0).wait_recv()
+                to_partner(0, q).wait_recv()
                 mine[q] = prob[1, q] + half[0, q]
                 to_across(q).start()
-        if step in (0, 2):
-            to_partner(step // 2).start()
-    to_partner(1).wait_recv()
-    for q in range(2):
+    for q in range(2):
+        to_partner(1, q).wait_recv()
         to_across(q).wait_recv()
         marg_ref[q] = ((prob[3, q] + half[1, q]) + part[q]) * 0.25
     for q in range(2):
-        to_partner(q).wait_send()
+        for n in range(2):
+            to_partner(n, q).wait_send()
         to_across(q).wait_send()
     returned(0, 0, r_send).wait()
     for step in STARTS:
@@ -395,7 +396,7 @@
             pltpu.VMEM((128, 256), bf16),
             pltpu.VMEM((256, 128), bf16),
             dma((3, 4)), dma((2,)), dma((2,)), dma((2,)), dma((2,)), dma((2, 4)), dma((2, 4)),
-            dma((2,)), dma((2,)), dma((2,)), dma((2,)),
+            dma((2, 2)), dma((2, 2)), dma((2,)), dma((2,)),
         ],
         compiler_params=pltpu.CompilerParams(
             collective_id=0, has_side_effects=True, vmem_limit_bytes=48 << 20

time: 48.9 us -> 48.7 us (level)
  no operation moved by 1% of the time
where the time goes in v6:
time: 48.7 us; the launch traced here: 48.6 us
  Pallas kernels  48 us (99%)
  between operations  0.64 us (1%)
    pallas_call x1, Pallas kernels, shards(): pl.pallas_call(kernel, name='walsh', out_shape=(jax.ShapeDtypeStruct((2,...  47 us
    pallas_call x1, Pallas kernels, shards(): pl.pallas_call(leave, name='leave', out_shape=(jax.ShapeDtypeStruct(out.s...  1.03 us

profile of v6, /device:TPU:1, one launch (start us, length us, event | category | flops | bytes accessed | tf_op | source)
XLA Modules:
  0.0 48.6 jit_solution(14683107302072446595)
XLA Ops:
  0.6 47.0 %walsh.1 = (f32[2,2,4,128,128]{4,3,2,1,0:T(8,128)S(1)}, f32[2,4,32,128]{3,2,1,0:T(8,128)S(1)}) custom-call(f32[2,2,4,128,128]{4,3,2,1,0:T(8,128)} %bitcast.4, f32[2,4,128,128]{3,2,1,0:T(8,128)} %bitcast.5, f32[2,128]{1,0:T(2,128)} %angle_ref.1), custom_call_target="tpu_custom_call" | custom-call | tf_op jit(solution)/shard_map/walsh/pallas_call | solution.py:370
  47.6 1.0 %leave.1 = (f32[2,2,4,128,128]{4,3,2,1,0:T(8,128)}, f32[2,4,32,128]{3,2,1,0:T(8,128)}) custom-call(f32[2,2,4,128,128]{4,3,2,1,0:T(8,128)S(1)} %get-tuple-element.6.values_ref, f32[2,4,32,128]{3,2,1,0:T(8,128)S(1)} %get-tuple-element.7.marginal_ref), custom_call_target="tpu_custom_call" | custom-call | tf_op jit(solution)/shard_map/leave/pallas_call | solution.py:409

commit v7 on v6

--- a/solution.py
+++ b/solution.py
@@ -310,10 +310,11 @@
             send_sem=d_send.at[n, q], recv_sem=d_recv.at[n, q], device_id=partner, device_id_type=LOGICAL,
         )
 
-    def to_across(q):
+    def to_across(q, pair):
+        ks = pl.ds(2 * pair, 2)
         return pltpu.make_async_remote_copy(
-            src_ref=mine.at[q], dst_ref=part.at[q],
-            send_sem=m_send.at[q], recv_sem=m_recv.at[q], device_id=across, device_id_type=LOGICAL,
+            src_ref=mine.at[q, ks], dst_ref=part.at[q, ks],
+            send_sem=m_send.at[q, pair], recv_sem=m_recv.at[q, pair], device_id=across, device_id_type=LOGICAL,
         )
 
     returned(0, 0, r_recv).wait()
@@ -337,16 +338,20 @@
                 to_partner(step // 2, q).start()
             if step == 1:
                 to_partner(0, q).wait_recv()
-                mine[q] = prob[1, q] + half[0, q]
-                to_across(q).start()
+                for pair in range(2):
+                    ks = slice(2 * pair, 2 * pair + 2)
+                    mine[q, ks] = prob[1, q, ks] + half[0, q, ks]
+                    to_across(q, pair).start()
     for q in range(2):
         to_partner(1, q).wait_recv()
-        to_across(q).wait_recv()
+        for pair in range(2):
+            to_across(q, pair).wait_recv()
         marg_ref[q] = ((prob[3, q] + half[1, q]) + part[q]) * 0.25
     for q in range(2):
         for n in range(2):
             to_partner(n, q).wait_send()
-        to_across(q).wait_send()
+        for pair in range(2):
+            to_across(q, pair).wait_send()
     returned(0, 0, r_send).wait()
     for step in STARTS:
         returned(1, step, r_send).wait()
@@ -396,7 +401,7 @@
             pltpu.VMEM((128, 256), bf16),
             pltpu.VMEM((256, 128), bf16),
             dma((3, 4)), dma((2,)), dma((2,)), dma((2,)), dma((2,)), dma((2, 4)), dma((2, 4)),
-            dma((2, 2)), dma((2, 2)), dma((2,)), dma((2,)),
+            dma((2, 2)), dma((2, 2)), dma((2, 2)), dma((2, 2)),
         ],
         compiler_params=pltpu.CompilerParams(
             collective_id=0, has_side_effects=True, vmem_limit_bytes=48 << 20

time: 48.7 us -> 48.8 us (level)
  no operation moved by 1% of the time
where the time goes in v7:
time: 48.8 us; the launch traced here: 48.7 us
  Pallas kernels  48 us (98%)
  between operations  0.64 us (1%)
    pallas_call x1, Pallas kernels, shards(): pl.pallas_call(kernel, name='walsh', out_shape=(jax.ShapeDtypeStruct((2,...  47 us
    pallas_call x1, Pallas kernels, shards(): pl.pallas_call(leave, name='leave', out_shape=(jax.ShapeDtypeStruct(out.s...  1.03 us

profile of v7, /device:TPU:1, one launch (start us, length us, event | category | flops | bytes accessed | tf_op | source)
XLA Modules:
  0.0 48.7 jit_solution(17934790297057776487)
XLA Ops:
  0.6 47.0 %walsh.1 = (f32[2,2,4,128,128]{4,3,2,1,0:T(8,128)S(1)}, f32[2,4,32,128]{3,2,1,0:T(8,128)S(1)}) custom-call(f32[2,2,4,128,128]{4,3,2,1,0:T(8,128)} %bitcast.4, f32[2,4,128,128]{3,2,1,0:T(8,128)} %bitcast.5, f32[2,128]{1,0:T(2,128)} %angle_ref.1), custom_call_target="tpu_custom_call" | custom-call | tf_op jit(solution)/shard_map/walsh/pallas_call | solution.py:375
  47.6 1.0 %leave.1 = (f32[2,2,4,128,128]{4,3,2,1,0:T(8,128)}, f32[2,4,32,128]{3,2,1,0:T(8,128)}) custom-call(f32[2,2,4,128,128]{4,3,2,1,0:T(8,128)S(1)} %get-tuple-element.6.values_ref, f32[2,4,32,128]{3,2,1,0:T(8,128)S(1)} %get-tuple-element.7.marginal_ref), custom_call_target="tpu_custom_call" | custom-call | tf_op jit(solution)/shard_map/leave/pallas_call | solution.py:414
